TPU v7x, 32 devices: a whole 2x2x4 slice. The times are simulated.
32 devices in a mesh: dp: 8 (over z, x), hyper: 4 (over y, core).
Axes of the slice: x: 2, y: 2, z: 4, core: 2. Of those that a mesh axis runs over, the one named last changes fastest.
Arguments:
- inputs: bfloat16 [64, 64, 128], P(('dp', 'hyper')), may hold values from -64 to 64
- labels: int32 [64, 64], P(('dp', 'hyper')), may hold values from 0 to 255
- client_ids: int32 [64], P(('dp', 'hyper')), may hold values from 0 to 63
- ext_weight: bfloat16 [128, 4096], replicated, may hold values from -0.5 to 0.5
- ext_bias: bfloat16 [4096], replicated, may hold values from -3 to 3
- embeddings: bfloat16 [64, 128], replicated, may hold values from -1.5 to 1.5
- hyper_in: bfloat16 [128, 50], replicated, may hold values from -2.09375 to 2.09375
- hyper_bias: float32 [50], replicated, may hold values from -3 to 3
- hyper_out: bfloat16 [4096, 50, 256], P('hyper'), may hold values from -0.1796875 to 0.1796875
Outputs:
- grad_ext_weight: float32 [128, 4096], replicated
- grad_ext_bias: float32 [4096], replicated
- grad_embeddings: float32 [64, 128], replicated
- grad_hyper_in: float32 [128, 50], replicated
- grad_hyper_bias: float32 [50], replicated
- grad_hyper_out: float32 [4096, 50, 256], P(('hyper', 'dp'))
Inputs may be any that keep to these rules, and one draw needn't show every extreme that they name: `client_ids`: A client may hold several slots or none.
All inputs are finite; a program needn't handle non-finite values.
Results may differ from a plain program's by a relative error of at most 0.014.
The roundings to bfloat16 on the way count: a program that leaves them out, or rounds other values in their place, can miss the bound.
Values may be sent and summed in bfloat16 or wider, within the bound.
A program may use at most 192 MiB of HBM per device.

v0:
```python
import jax
import jax.numpy as jnp
from jax import lax
from jax.sharding import PartitionSpec as P

highest = lax.Precision.HIGHEST
f32 = jnp.float32
bf16 = jnp.bfloat16


def silu_slope(values):
    logistic = jax.nn.sigmoid(values)
    return logistic * (1.0 + values * (1.0 - logistic))


def class_grads(logits, slot_labels, row_count):
    largest = jnp.max(logits, axis=-1, keepdims=True)
    exponent = jnp.exp(logits - largest)
    probability = exponent / jnp.sum(exponent, axis=-1, keepdims=True)
    classes = jnp.arange(logits.shape[-1], dtype=jnp.int32)
    onehot = (slot_labels[..., None] == classes).astype(f32)
    return ((probability - onehot) / row_count).astype(bf16)


def local(
    inputs, labels, client_ids, ext_weight, ext_bias, embeddings, hyper_in, hyper_bias, hyper_out
):
    everyone = ("dp", "hyper")
    n_dp, n_hyper = (lax.axis_size("dp"), lax.axis_size("hyper"))
    i, j = (lax.axis_index("dp"), lax.axis_index("hyper"))
    own, rows, width_in = inputs.shape
    wide = hyper_out.shape[0]
    narrow = wide // n_dp
    group = own * n_hyper
    slots = group * n_dp
    classes = hyper_out.shape[2]
    ids = lax.all_gather(client_ids, everyone, axis=0, tiled=True)
    in_group = lax.all_gather(inputs, "hyper", axis=0, tiled=True)
    in_all = lax.all_gather(in_group, "dp", axis=0, tiled=True)
    select = ids[:, None] == jnp.arange(embeddings.shape[0], dtype=jnp.int32)[None, :]
    picked = jnp.dot(select.astype(bf16), embeddings, preferred_element_type=f32).astype(bf16)
    hyper_preact = jnp.dot(picked, hyper_in, preferred_element_type=f32) + hyper_bias
    hidden = jax.nn.silu(hyper_preact).astype(bf16)
    w_wide = lax.dynamic_slice_in_dim(ext_weight, j * wide, wide, 1)
    b_wide = lax.dynamic_slice_in_dim(ext_bias, j * wide, wide, 0).astype(f32)
    preact = jnp.dot(in_group.reshape(group * rows, width_in), w_wide, preferred_element_type=f32)
    features = jax.nn.silu(preact + b_wide).astype(bf16).reshape(group, rows, wide)
    hidden_group = lax.dynamic_slice_in_dim(hidden, i * group, group, 0)
    heads = jnp.einsum("kh,dhc->kdc", hidden_group, hyper_out, preferred_element_type=f32)
    part = jnp.einsum("krd,kdc->krc", features, heads.astype(bf16), preferred_element_type=f32)
    parts = lax.all_to_all(
        part.reshape(n_hyper, own * rows, classes), "hyper", split_axis=0, concat_axis=0
    )
    logits = jnp.sum(parts, axis=0).reshape(own, rows, classes)
    dlogits = class_grads(logits, labels, rows)
    dl_all = lax.all_gather(dlogits, everyone, axis=0, tiled=True)
    start = (j * n_dp + i) * narrow
    w = lax.dynamic_slice_in_dim(ext_weight, start, narrow, 1)
    b = lax.dynamic_slice_in_dim(ext_bias, start, narrow, 0).astype(f32)
    out_rows = lax.dynamic_slice_in_dim(hyper_out, i * narrow, narrow, 0)
    flat = in_all.reshape(slots * rows, width_in)
    preact = jnp.dot(flat, w, preferred_element_type=f32) + b
    features = jax.nn.silu(preact).astype(bf16).reshape(slots, rows, narrow)
    heads = jnp.einsum("kh,dhc->kdc", hidden, out_rows, preferred_element_type=f32).astype(bf16)
    dheads = jnp.einsum("krd,krc->kdc", features, dl_all, preferred_element_type=f32).astype(bf16)
    dfeatures = jnp.einsum("krc,kdc->krd", dl_all, heads, preferred_element_type=f32).astype(bf16)
    dpreact = (dfeatures.reshape(slots * rows, narrow).astype(f32) * silu_slope(preact)).astype(
        bf16
    )
    grad_weight = jnp.dot(flat.T, dpreact, preferred_element_type=f32)
    grad_bias = jnp.sum(dpreact.astype(f32), axis=0)
    grad_out = jnp.einsum("kh,kdc->dhc", hidden, dheads, preferred_element_type=f32)
    dhidden = jnp.einsum("kdc,dhc->kh", dheads, out_rows, preferred_element_type=f32)
    dhidden = lax.psum(dhidden, everyone)
    hyper_dpre = dhidden * silu_slope(hyper_preact)
    grad_in = jnp.dot(picked.astype(f32).T, hyper_dpre, precision=highest)
    grad_hbias = jnp.sum(hyper_dpre, axis=0)
    back_rows = jnp.dot(hyper_dpre, hyper_in.astype(f32).T, precision=highest)
    grad_table = jnp.dot(select.astype(f32).T, back_rows, precision=highest)
    both = jnp.concatenate([grad_weight, grad_bias[None]], axis=0)
    both = lax.all_gather(both, ("hyper", "dp"), axis=1, tiled=True)
    return (both[:-1], both[-1], grad_table, grad_in, grad_hbias, grad_out)


def solution(mesh):
    placed = (
        P(("dp", "hyper"), None, None),
        P(("dp", "hyper"), None),
        P(("dp", "hyper")),
        P(),
        P(),
        P(),
        P(),
        P(),
        P("hyper", None, None),
    )
    return jax.shard_map(
        local,
        mesh=mesh,
        in_specs=placed,
        out_specs=(P(), P(), P(), P(), P(), P(("hyper", "dp"), None, None)),
        check_vma=False,
    )
```

profile of v0, /device:TPU:0, one launch (start us, length us, event | category | flops | bytes accessed | tf_op | source)
XLA Modules:
  0.0 276.0 jit_solution(7571744221663631513)
XLA Ops:
  7.2 0.0 copy-start
  7.2 0.0 all-gather.4.cloned.1.call-start
  7.2 0.9 dynamic-update-slice
  8.2 42.0 %all-reduce = s32[64]{0:T(128)S(1)} all-reduce(s32[64]{0:T(128)S(1)} %dynamic-update-slice), channel_id=1, replica_groups=mesh['dp'=8,'hyper'=4] {'dp','hyper'}, use_global_device_ids=true, to_apply=%add | all-reduce | flops 64 | bytes 512
  50.1 6.0 %all_gather.15 = bf16[8,64,128]{2,1,0:T(8,128)(2,1)S(1)} all-gather(bf16[2,64,128]{2,1,0:T(8,128)(2,1)} %param.9), channel_id=1, replica_groups=mesh['dp'=8,'hyper'=4] {'hyper'}, dimensions={0}, use_global_device_ids=true | all-gather | bytes 163840 | tf_op jit(solution)/shard_map/all_gather | solution.py:38
  56.1 0.0 copy-start.3
  56.1 0.7 dynamic-slice_convert_fusion
  56.8 0.9 convolution_convert_fusion.2
  57.7 0.9 multiply_convert_fusion.3
  58.6 0.0 copy-done
  58.6 0.7 fusion.21
  59.4 0.0 copy-done.3
  59.4 28.0 %convolution_convert_fusion.1 = bf16[8,1024,256]{2,0,1:T(8,128)(2,1)S(1)} fusion(bf16[64,50]{0,1:T(8,128)(2,1)S(1)} %get-tuple-element.29, s32[]{:T(128)S(6)} %select_n.15, bf16[1024,50,256]{2,0,1:T(8,128)(2,1)} %param.17), kind=kOutput, calls=%fused_computation.16 | convolution fusion | flops 211812352 | bytes 30415108 | tf_op jit(solution)/shard_map/kh,dhc->kdc/dot_general | solution.py:49
  87.4 0.0 copy-start.5
  87.4 0.9 fusion.3
  88.2 11.8 %all_to_all.5 = f32[4,128,256]{2,1,0:T(8,128)S(1)} all-to-all(f32[4,128,256]{2,1,0:T(8,128)S(1)} %bitcast.61), channel_id=1, replica_groups=mesh['dp'=8,'hyper'=4] {'hyper'}, dimensions={0} | all-to-all | bytes 1048576 | tf_op jit(solution)/shard_map/all_to_all | solution.py:51
  100.0 0.1 reduce_max.9
  100.1 0.2 exponential_reduce_fusion
  100.3 0.1 sub.24
  100.4 0.1 div.32
  100.5 0.0 copy-done.5
  100.5 0.8 multiply_convert_fusion.2
  101.3 0.0 all-gather.4.cloned.1.call-update
  101.3 0.0 all-gather.6.cloned.1.call-start
  101.3 0.7 all-gather.6.cloned.1.call-update
  102.0 0.0 all-gather.8.cloned.1.call-start
  102.1 27.8 %copy.28 = bf16[1024,50,256]{2,1,0:T(8,128)(2,1)} copy(bf16[1024,50,256]{2,0,1:T(8,128)(2,1)} %param.17) | data formatting | bytes 52428800 | tf_op args[8]
  129.9 0.8 dynamic-slice_convert_fusion.1
  130.6 5.3 %fusion.15 = bf16[64,128,256]{2,0,1:T(8,128)(2,1)} fusion(bf16[1024,50,256]{2,1,0:T(8,128)(2,1)} %copy.28, s32[]{:T(128)S(6)} %select_n.16, bf16[64,50]{0,1:T(8,128)(2,1)S(1)} %get-tuple-element.29), kind=kOutput, calls=%fused_computation.14 | convolution fusion | flops 211812352 | bytes 7870724 | tf_op jit(solution)/shard_map/kh,dhc->kdc/dot_general | solution.py:64
  136.0 20.6 %all-gather.4.cloned.1.call-done = bf16[64,64,256]{2,1,0:T(8,128)(2,1)} async-done(((bf16[2,64,256]{2,1,0:T(8,128)(2,1)}), bf16[64,64,256]{2,1,0:T(8,128)(2,1)}) %all-gather.4.cloned.1.call-update) | async-done | bytes 2097168 | tf_op jit(solution)/shard_map/all_gather | solution.py:56
  156.5 5.5 %fusion.22 = bf16[64,64,128]{2,1,0:T(8,128)(2,1)S(1)} fusion(bf16[64,64,256]{2,1,0:T(8,128)(2,1)} %all-gather.4.cloned.1.call-done, bf16[64,128,256]{2,0,1:T(8,128)(2,1)} %fusion.15), kind=kOutput, calls=%fused_computation.27 | convolution fusion | flops 268959744 | bytes 7340032 | tf_op jit(solution)/shard_map/krc,kdc->krd/dot_general | solution.py:66
  162.1 0.2 bitcast_convert_fusion
  162.3 1.8 copy.32
  164.1 33.7 %all-gather.6.cloned.1.call-done = bf16[64,64,128]{2,1,0:T(8,128)(2,1)} async-done(((bf16[8,64,128]{2,1,0:T(8,128)(2,1)}), bf16[64,64,128]{2,1,0:T(8,128)(2,1)}) %all-gather.6.cloned.1.call-update) | async-done | bytes 1048592 | tf_op jit(solution)/shard_map/all_gather | solution.py:39
  197.8 0.0 copy-start.2
  197.8 4.2 %convert_reduce_fusion = (f32[128]{0:T(128)S(1)}, bf16[4096,128]{0,1:T(8,128)(2,1)S(1)}, bf16[4096,128]{0,1:T(8,128)(2,1)}) fusion(f32[4096,128]{0,1:T(8,128)} %copy.32, f32[128]{0:T(128)S(1)} %dynamic-slice_convert_fusion.1, bf16[4096,128]{1,0:T(8,128)(2,1)} %bitcast.58, bf16[128,4096]{1,0:T(8,128)(2,1)S(1)} %copy-done, s32[]{:T(128)S(6)} %select_n.17), kind=kOutput, calls=%fused_computation.23 | convolution fusion | flops 141557632 | bytes 5276676 | tf_op jit(solution)/shard_map/dot_general | solution.py:62
  202.1 0.0 copy-start.1
  202.1 0.0 copy-done.2
  202.1 0.5 convolution_bitcast_fusion
  202.6 0.6 pad_maximum_fusion
  203.2 0.0 all-gather.8.cloned.1.call-update
  203.2 2.3 copy.33
  205.5 0.0 copy-done.1
  205.5 2.5 convolution_convert_fusion
  208.0 3.3 %fusion.12 = f32[128,50,256]{2,1,0:T(8,128)S(1)} fusion(bf16[64,128,256]{2,1,0:T(8,128)(2,1)S(1)} %convolution_convert_fusion, bf16[64,50]{0,1:T(8,128)(2,1)S(1)} %get-tuple-element.29), kind=kOutput, calls=%fused_computation.13 | convolution fusion | flops 209715200 | bytes 10754304 | tf_op jit(solution)/shard_map/kh,kdc->dhc/dot_general | solution.py:72
  211.3 4.8 %copy.37 = f32[128,50,256]{2,0,1:T(8,128)} copy(f32[128,50,256]{2,1,0:T(8,128)S(1)} %fusion.12) | data formatting | bytes 13107200
  216.1 0.0 copy-start.4
  216.1 7.1 %fusion.25 = f32[64,50]{0,1:T(8,128)S(1)} fusion(bf16[1024,50,256]{2,1,0:T(8,128)(2,1)} %copy.28, s32[]{:T(128)S(6)} %select_n.16, bf16[64,128,256]{2,1,0:T(8,128)(2,1)S(1)} %convolution_convert_fusion), kind=kOutput, calls=%fused_computation.29 | convolution fusion | flops 209715200 | bytes 7877124 | tf_op jit(solution)/shard_map/kdc,dhc->kh/dot_general | solution.py:73
  223.2 39.1 %psum.7 = f32[64,50]{0,1:T(8,128)S(1)} all-reduce(f32[64,50]{0,1:T(8,128)S(1)} %fusion.25), channel_id=1, replica_groups=mesh['dp'=8,'hyper'=4] {'dp','hyper'}, use_global_device_ids=true, to_apply=%region_4.5 | all-reduce | flops 3200 | bytes 25600 | tf_op jit(solution)/shard_map/psum | solution.py:74
  262.3 0.6 fusion.45
  263.0 0.0 copy-done.4
  263.0 0.2 fusion.46
  263.2 0.9 fusion.32
  264.1 0.8 fusion.47
  264.9 0.0 all-gather.8.cloned.1.call-done
  264.9 1.5 slice.9
  266.4 3.1 %slice.8 = f32[128,4096]{1,0:T(8,128)} slice(f32[129,4096]{1,0:T(8,128)} %all-gather.8.cloned.1.call-done), slice={[0:128], [0:4096]} | slice | bytes 4194304 | tf_op jit(solution)/shard_map/slice | solution.py:82
  (2 shorter events, 0.0 us)
Async XLA Ops:
  7.2 51.5 %copy-start = (bf16[128,4096]{1,0:T(8,128)(2,1)S(1)}, bf16[128,4096]{1,0:T(8,128)(2,1)}, u32[]{:S(2)}) copy-start(bf16[128,4096]{1,0:T(8,128)(2,1)} %param.12) | copy-start | bytes 3145732
  7.2 149.4 %all-gather.4.cloned.1.call-start = ((), (), s32[]{:S(2)}) async-start(), calls=%async_computation.1 | async-start | bytes 2162688 | tf_op jit(solution)/shard_map/all_gather | solution.py:56
  56.1 3.2 %copy-start.3 = (bf16[8,64,128]{2,1,0:T(8,128)(2,1)}, bf16[8,64,128]{2,1,0:T(8,128)(2,1)S(1)}, u32[]{:S(2)}) copy-start(bf16[8,64,128]{2,1,0:T(8,128)(2,1)S(1)} %all_gather.15) | copy-start | bytes 393220
  87.4 13.1 %copy-start.5 = (s32[2,64]{1,0:T(2,128)S(1)}, s32[2,64]{1,0:T(2,128)}, u32[]{:S(2)}) copy-start(s32[2,64]{1,0:T(2,128)} %param.10) | copy-start | bytes 1540
  101.3 96.5 %all-gather.6.cloned.1.call-start = ((), (), s32[]{:S(2)}) async-start(), calls=%async_computation.2 | async-start | bytes 1179648 | tf_op jit(solution)/shard_map/all_gather | solution.py:39
  102.0 162.8 %all-gather.8.cloned.1.call-start = ((), (), s32[]{:S(2)}) async-start(), calls=%async_computation.3 | async-start | bytes 2297856 | tf_op jit(solution)/shard_map/all_gather | solution.py:81
  197.8 4.2 %copy-start.2 = (bf16[64,64,128]{2,1,0:T(8,128)(2,1)S(1)}, bf16[64,64,128]{2,1,0:T(8,128)(2,1)}, u32[]{:S(2)}) copy-start(bf16[64,64,128]{2,1,0:T(8,128)(2,1)} %all-gather.6.cloned.1.call-done) | copy-start | bytes 3145732
  202.1 3.4 %copy-start.1 = (bf16[64,64,256]{2,1,0:T(8,128)(2,1)S(1)}, bf16[64,64,256]{2,1,0:T(8,128)(2,1)}, u32[]{:S(2)}) copy-start(bf16[64,64,256]{2,1,0:T(8,128)(2,1)} %all-gather.4.cloned.1.call-done) | copy-start | bytes 6291460
  216.1 46.9 %copy-start.4 = (bf16[128,50]{0,1:T(8,128)(2,1)S(1)}, bf16[128,50]{0,1:T(8,128)(2,1)}, u32[]{:S(2)}) copy-start(bf16[128,50]{0,1:T(8,128)(2,1)} %param.15) | copy-start | bytes 38404
Sparse Core Ops, SparseCore 0:
  101.4 55.0 all-gather.3
  158.7 39.1 all-gather.5
  203.4 56.2 all-gather.7
where the time goes:
time: 277 us; the launch traced here: 276 us
  blocking collectives  98.8 us (36%)
  matrix products  61.7 us (22%)
  waiting for transfers between devices  55.1 us (20%)
  local copies, waits for them, and re-layouts  42.4 us (15%)
  between operations  13.9 us (5%)
  other arithmetic  4 us (1%)
    unnamed x1, blocking collectives  42 us
    psum x1, blocking collectives, local(): dhidden = lax.psum(dhidden, everyone)  39.1 us
    all_gather x1, waiting for transfers between devices, local(): in_all = lax.all_gather(in_group, 'dp', axis=0, tiled=True)  33.7 us
    unnamed x16, local copies, waits for them, and re-layouts  33.5 us
    dot_general x1, matrix products, local(): jnp.einsum('kh,dhc->kdc', hidden_group, hyper_out, preferred_element_type...  28 us
    all_gather x1, waiting for transfers between devices, local(): dl_all = lax.all_gather(dlogits, everyone, axis=0, tiled=True)  20.6 us
    all_to_all x1, blocking collectives, local(): lax.all_to_all(part.reshape(n_hyper, own * rows, classes), 'hyper', split...  11.8 us
    dot_general x1, matrix products, local(): jnp.einsum('kdc,dhc->kh', dheads, out_rows, preferred_element_type=f32)  7.1 us
  transfers between devices with their start and end apart: 3, of which 2 were waited for; matrix products, arithmetic and copies ran while one was open for 23% of the time, Pallas kernels for 0%

commit v1 on v0

--- a/solution.py
+++ b/solution.py
@@ -2,10 +2,29 @@
 import jax.numpy as jnp
 from jax import lax
 from jax.sharding import PartitionSpec as P
+from jax.lax import axis_index, axis_size, ppermute
 
 highest = lax.Precision.HIGHEST
 f32 = jnp.float32
 bf16 = jnp.bfloat16
+
+
+def handle_stops_all(block_in, out_dim):
+    carry_out = list(block_in.shape[1:])
+    carry_out[out_dim] *= block_in.shape[0]
+    shaped = jnp.moveaxis(block_in, 0, out_dim).reshape(carry_out)
+    return shaped
+
+
+def islands_obtain(local_block, net_axis):
+    lower, long_array = (axis_size(net_axis), axis_index(net_axis))
+    aux, r1 = (local_block[None], 1)
+    while r1 < lower:
+        last = ppermute(aux, net_axis, tuple(((dev_i, dev_i ^ r1) for dev_i in range(lower))))
+        v_next = long_array & r1 == 0
+        aux = jnp.concatenate([jnp.where(v_next, aux, last), jnp.where(v_next, last, aux)])
+        r1 *= 2
+    return aux
 
 
 def silu_slope(values):
@@ -36,7 +55,7 @@
     classes = hyper_out.shape[2]
     ids = lax.all_gather(client_ids, everyone, axis=0, tiled=True)
     in_group = lax.all_gather(inputs, "hyper", axis=0, tiled=True)
-    in_all = lax.all_gather(in_group, "dp", axis=0, tiled=True)
+    in_all = handle_stops_all(islands_obtain(in_group, "dp"), 0)
     select = ids[:, None] == jnp.arange(embeddings.shape[0], dtype=jnp.int32)[None, :]
     picked = jnp.dot(select.astype(bf16), embeddings, preferred_element_type=f32).astype(bf16)
     hyper_preact = jnp.dot(picked, hyper_in, preferred_element_type=f32) + hyper_bias

time: 277 us -> 262 us (0.946)
  local copies, waits for them, and re-layouts: 42.4 us -> 25.6 us
  starting transfers between devices: 0.12 us -> 5.63 us
  matrix products: 61.7 us -> 58.7 us
    all_gather x1 -> x0, waiting for transfers between devices: 33.7 us -> none  [local(): in_all = lax.all_gather(in_group, 'dp', axis=0, tiled=True)]
    ppermute x0 -> x3, waiting for transfers between devices: none -> 22.5 us  [islands_obtain(): ppermute(aux, net_axis, tuple(((dev_i, dev_i ^ r1) for dev_i in range(low...]
    unnamed x16 -> x22, local copies, waits for them, and re-layouts: 33.5 us -> 12.1 us
    all_gather x1, waiting for transfers between devices: 20.6 us -> 29.9 us  [local(): dl_all = lax.all_gather(dlogits, everyone, axis=0, tiled=True)]
    dot_general x1, matrix products: 7.1 us -> 1.26 us  [local(): jnp.einsum('kdc,dhc->kh', dheads, out_rows, preferred_element_type=f32)]
    ppermute x0 -> x3, starting transfers between devices: none -> 5.55 us  [islands_obtain(): ppermute(aux, net_axis, tuple(((dev_i, dev_i ^ r1) for dev_i in range(low...]
    convert_element_type x2 -> x1, local copies, waits for them, and re-layouts: 4.08 us -> 6.54 us  [local(): jnp.einsum('krd,krc->kdc', features, dl_all, preferred_element_type=f32)]
  transfers between devices with their start and end apart: 3 -> 5, of which waited for: 2 -> 4; matrix products, arithmetic and copies ran while one was open for 23% -> 15% of each run, Pallas kernels for 0% -> 0%
where the time goes in v1:
time: 262 us; the launch traced here: 261 us
  blocking collectives  100 us (38%)
  matrix products  58.7 us (22%)
  waiting for transfers between devices  52.5 us (20%)
  local copies, waits for them, and re-layouts  25.6 us (10%)
  between operations  14.2 us (5%)
  starting transfers between devices  5.63 us (2%)
  other arithmetic  4.11 us (2%)
    unnamed x1, blocking collectives  42 us
    psum x1, blocking collectives, local(): dhidden = lax.psum(dhidden, everyone)  40.4 us
    all_gather x1, waiting for transfers between devices, local(): dl_all = lax.all_gather(dlogits, everyone, axis=0, tiled=True)  29.9 us
    dot_general x1, matrix products, local(): jnp.einsum('kh,dhc->kdc', hidden_group, hyper_out, preferred_element_type...  27.9 us
    ppermute x3, waiting for transfers between devices, islands_obtain(): ppermute(aux, net_axis, tuple(((dev_i, dev_i ^ r1) for dev_i in range(low...  22.5 us
    unnamed x22, local copies, waits for them, and re-layouts  12.1 us
    all_to_all x1, blocking collectives, local(): lax.all_to_all(part.reshape(n_hyper, own * rows, classes), 'hyper', split...  11.8 us
    convert_element_type x1, local copies, waits for them, and re-layouts, local(): jnp.einsum('krd,krc->kdc', features, dl_all, preferred_element_type=f32)  6.54 us
  transfers between devices with their start and end apart: 5, of which 4 were waited for; matrix products, arithmetic and copies ran while one was open for 15% of the time, Pallas kernels for 0%

profile of v1, /device:TPU:0, one launch (start us, length us, event | category | flops | bytes accessed | tf_op | source)
XLA Modules:
  0.0 260.9 jit_solution(16603999730346661471)
XLA Ops:
  7.2 0.0 copy-start
  7.2 0.0 all-gather.3.cloned.1.call-start
  7.2 0.9 dynamic-update-slice
  8.2 42.0 %all-reduce = s32[64]{0:T(128)S(1)} all-reduce(s32[64]{0:T(128)S(1)} %dynamic-update-slice), channel_id=1, replica_groups=mesh['dp'=8,'hyper'=4] {'dp','hyper'}, use_global_device_ids=true, to_apply=%add | all-reduce | flops 64 | bytes 512
  50.1 6.0 %all_gather.12 = bf16[8,64,128]{2,1,0:T(8,128)(2,1)S(1)} all-gather(bf16[2,64,128]{2,1,0:T(8,128)(2,1)} %param.9), channel_id=1, replica_groups=mesh['dp'=8,'hyper'=4] {'hyper'}, dimensions={0}, use_global_device_ids=true | all-gather | bytes 163840 | tf_op jit(solution)/shard_map/all_gather | solution.py:57
  56.2 0.7 dynamic-slice_convert_fusion
  56.8 0.9 convolution_convert_fusion.1
  57.7 0.9 multiply_convert_fusion.2
  58.6 0.0 copy-done
  58.6 1.7 fusion.15
  60.3 27.9 %fusion = bf16[8,1024,256]{2,0,1:T(8,128)(2,1)S(1)} fusion(bf16[1024,50,256]{2,0,1:T(8,128)(2,1)} %param.17, bf16[64,50]{0,1:T(8,128)(2,1)S(1)} %get-tuple-element.29, s32[]{:T(128)S(6)} %select_n.60), kind=kOutput, calls=%fused_computation | convolution fusion | flops 209715200 | bytes 30415108 | tf_op jit(solution)/shard_map/kh,dhc->kdc/dot_general | solution.py:68
  88.2 0.0 copy-start.8
  88.2 2.1 fusion.2
  90.3 11.8 %all_to_all.5 = f32[4,128,256]{2,1,0:T(8,128)S(1)} all-to-all(f32[4,128,256]{2,1,0:T(8,128)S(1)} %bitcast.64), channel_id=1, replica_groups=mesh['dp'=8,'hyper'=4] {'hyper'}, dimensions={0} | all-to-all | bytes 1048576 | tf_op jit(solution)/shard_map/all_to_all | solution.py:70
  102.1 0.1 reduce_max.9
  102.2 0.2 exponential_reduce_fusion
  102.4 0.1 sub.24
  102.5 0.1 div.32
  102.6 0.0 copy-done.8
  102.6 0.8 multiply_convert_fusion.1
  103.4 0.0 all-gather.3.cloned.1.call-update
  103.4 0.0 all-gather.5.cloned.1.call-start
  103.4 1.4 collective-permute-start
  104.8 3.6 %collective-permute-done = bf16[1,8,64,128]{3,2,1,0:T(8,128)(2,1)S(1)} collective-permute-done((bf16[1,8,64,128]{3,2,1,0:T(8,128)(2,1)S(1)}, bf16[1,8,64,128]{3,2,1,0:T(8,128)(2,1)S(1)}, u32[]{:S(2)}, u32[]{:S(2)}) %collective-permute-start) | collective-permute-done | bytes 131104 | tf_op jit(solution)/shard_map/ppermute | solution.py:23
  108.5 1.6 collective-permute-start.1
  110.1 2.2 constant_dynamic-slice_fusion
  112.3 0.0 copy-start.2
  112.3 3.3 %collective-permute-done.1 = bf16[2,8,64,128]{3,2,1,0:T(8,128)(2,1)S(1)} collective-permute-done((bf16[2,8,64,128]{3,2,1,0:T(8,128)(2,1)S(1)}, bf16[2,8,64,128]{3,2,1,0:T(8,128)(2,1)S(1)}, u32[]{:S(2)}, u32[]{:S(2)}) %collective-permute-start.1) | collective-permute-done | bytes 262176 | tf_op jit(solution)/shard_map/ppermute | solution.py:23
  115.7 2.6 collective-permute-start.2
  118.2 0.8 dynamic-slice_convert_fusion.1
  119.0 5.1 %fusion.6 = bf16[64,128,256]{2,0,1:T(8,128)(2,1)} fusion(bf16[128,50,256]{2,0,1:T(8,128)(2,1)S(1)} %constant_dynamic-slice_fusion, bf16[64,50]{0,1:T(8,128)(2,1)S(1)} %get-tuple-element.29), kind=kOutput, calls=%fused_computation.9 | convolution fusion | flops 209715200 | bytes 7477504 | tf_op jit(solution)/shard_map/kh,dhc->kdc/dot_general | solution.py:83
  124.1 0.0 copy-done.2
  124.1 15.6 %collective-permute-done.2 = bf16[4,8,64,128]{3,2,1,0:T(8,128)(2,1)S(1)} collective-permute-done((bf16[4,8,64,128]{3,2,1,0:T(8,128)(2,1)S(1)}, bf16[4,8,64,128]{3,2,1,0:T(8,128)(2,1)S(1)}, u32[]{:S(2)}, u32[]{:S(2)}) %collective-permute-start.2) | collective-permute-done | bytes 524320 | tf_op jit(solution)/shard_map/ppermute | solution.py:23
  139.7 0.1 broadcast_select_fusion.1
  139.8 0.1 pad_maximum_fusion
  139.9 29.9 %all-gather.3.cloned.1.call-done = bf16[64,64,256]{2,1,0:T(8,128)(2,1)} async-done(((bf16[2,64,256]{2,1,0:T(8,128)(2,1)}), bf16[64,64,256]{2,1,0:T(8,128)(2,1)}) %all-gather.3.cloned.1.call-update) | async-done | bytes 2097168 | tf_op jit(solution)/shard_map/all_gather | solution.py:75
  169.8 5.5 %fusion.16 = bf16[64,64,128]{2,1,0:T(8,128)(2,1)S(1)} fusion(bf16[64,64,256]{2,1,0:T(8,128)(2,1)} %all-gather.3.cloned.1.call-done, bf16[64,128,256]{2,0,1:T(8,128)(2,1)} %fusion.6), kind=kOutput, calls=%fused_computation.24 | convolution fusion | flops 268959744 | bytes 7340032 | tf_op jit(solution)/shard_map/krc,kdc->krd/dot_general | solution.py:85
  175.3 2.3 convert_reduce_fusion
  177.6 0.5 fusion.31
  178.1 0.6 pad_maximum_fusion.3
  178.8 0.0 all-gather.5.cloned.1.call-update
  178.8 0.0 copy-start.5
  178.8 0.0 copy-start.6
  178.8 6.4 %copy.27 = bf16[128,50,256]{0,1,2:T(8,128)(2,1)} copy(bf16[128,50,256]{2,0,1:T(8,128)(2,1)} %copy-done.2) | data formatting | bytes 6553600
  185.2 0.0 copy-done.5
  185.2 0.0 copy-done.6
  185.2 3.3 %convolution_convert_fusion = bf16[64,128,256]{2,1,0:T(8,128)(2,1)} fusion(bf16[64,64,128]{2,1,0:T(8,128)(2,1)S(1)} %bitcast.61, bf16[64,64,256]{2,1,0:T(8,128)(2,1)S(1)} %copy-done.5), kind=kOutput, calls=%fused_computation.12 | convolution fusion | flops 270532608 | bytes 7340032 | tf_op jit(solution)/shard_map/krd,krc->kdc/dot_general | solution.py:84
  188.5 6.5 %copy.20 = bf16[64,128,256]{1,0,2:T(8,128)(2,1)} copy(bf16[64,128,256]{2,1,0:T(8,128)(2,1)} %convolution_convert_fusion) | data formatting | bytes 8388608 | tf_op jit(solution)/shard_map/convert_element_type | solution.py:84
  195.0 5.4 %fusion.8 = f32[128,50,256]{2,1,0:T(8,128)S(1)} fusion(bf16[64,128,256]{2,1,0:T(8,128)(2,1)} %convolution_convert_fusion, bf16[64,50]{0,1:T(8,128)(2,1)S(1)} %get-tuple-element.29), kind=kOutput, calls=%fused_computation.11 | convolution fusion | flops 209715200 | bytes 10754304 | tf_op jit(solution)/shard_map/kh,kdc->dhc/dot_general | solution.py:91
  200.5 0.0 copy-start.3
  200.5 0.0 copy-start.4
  200.5 4.8 %copy.22 = f32[128,50,256]{2,0,1:T(8,128)} copy(f32[128,50,256]{2,1,0:T(8,128)S(1)} %fusion.8) | data formatting | bytes 13107200
  205.3 0.0 copy-done.3
  205.3 0.0 copy-done.4
  205.3 1.3 convolution_bitcast_fusion
  206.5 40.4 %psum.7 = f32[64,50]{0,1:T(8,128)S(1)} all-reduce(f32[64,50]{0,1:T(8,128)S(1)} %convolution_bitcast_fusion), channel_id=1, replica_groups=mesh['dp'=8,'hyper'=4] {'dp','hyper'}, use_global_device_ids=true, to_apply=%region_4.5 | all-reduce | flops 3200 | bytes 25600 | tf_op jit(solution)/shard_map/psum | solution.py:93
  246.9 0.6 fusion.29
  247.6 0.0 copy-done.7
  247.6 0.2 fusion.32
  247.8 0.9 fusion.19
  248.7 0.8 fusion.33
  249.5 1.5 slice.9
  251.0 3.1 %slice.8 = f32[128,4096]{1,0:T(8,128)} slice(f32[129,4096]{1,0:T(8,128)} %all-gather.5.cloned.1.call-done), slice={[0:128], [0:4096]} | slice | bytes 4194304 | tf_op jit(solution)/shard_map/slice | solution.py:101
  254.1 0.0 copy-done.1
  (9 shorter events, 0.2 us)
Async XLA Ops:
  7.2 51.5 %copy-start = (bf16[128,4096]{1,0:T(8,128)(2,1)S(1)}, bf16[128,4096]{1,0:T(8,128)(2,1)}, u32[]{:S(2)}) copy-start(bf16[128,4096]{1,0:T(8,128)(2,1)} %param.12) | copy-start | bytes 3145732
  7.2 162.6 %all-gather.3.cloned.1.call-start = ((), (), s32[]{:S(2)}) async-start(), calls=%async_computation.1 | async-start | bytes 2162688 | tf_op jit(solution)/shard_map/all_gather | solution.py:75
  88.2 14.4 %copy-start.8 = (s32[2,64]{1,0:T(2,128)S(1)}, s32[2,64]{1,0:T(2,128)}, u32[]{:S(2)}) copy-start(s32[2,64]{1,0:T(2,128)} %param.10) | copy-start | bytes 1540
  103.4 146.1 %all-gather.5.cloned.1.call-start = ((), (), s32[]{:S(2)}) async-start(), calls=%async_computation.2 | async-start | bytes 2297856 | tf_op jit(solution)/shard_map/all_gather | solution.py:100
  103.4 5.0 %collective-permute-start = (bf16[1,8,64,128]{3,2,1,0:T(8,128)(2,1)S(1)}, bf16[1,8,64,128]{3,2,1,0:T(8,128)(2,1)S(1)}, u32[]{:S(2)}, u32[]{:S(2)}) collective-permute-start(bf16[1,8,64,128]{3,2,1,0:T(8,128)(2,1)S(1)} %bitcast.63), channel_id=1, source_target_pairs={{0,4},{4,0},{8,12},{12,8},{16,20},{20,16},{24,28},{28,24},{1,5},{5... | collective-permute-start | bytes 393224 | tf_op jit(solution)/shard_map/ppermute | solution.py:23
  108.5 7.0 %collective-permute-start.1 = (bf16[2,8,64,128]{3,2,1,0:T(8,128)(2,1)S(1)}, bf16[2,8,64,128]{3,2,1,0:T(8,128)(2,1)S(1)}, u32[]{:S(2)}, u32[]{:S(2)}) collective-permute-start(bf16[2,8,64,128]{3,2,1,0:T(8,128)(2,1)S(1)} %pad_maximum_fusion.2), channel_id=1, source_target_pairs={{0,8},{4,12},{8,0},{12,4},{16,24},{20,28},{24,16},{28,20},{1,9},{5... | collective-permute-start | bytes 786440 | tf_op jit(solution)/shard_map/ppermute | solution.py:23
  112.3 11.8 %copy-start.2 = (bf16[128,50,256]{2,0,1:T(8,128)(2,1)}, bf16[128,50,256]{2,0,1:T(8,128)(2,1)S(1)}, u32[]{:S(2)}) copy-start(bf16[128,50,256]{2,0,1:T(8,128)(2,1)S(1)} %constant_dynamic-slice_fusion) | copy-start | bytes 9830404
  115.7 24.0 %collective-permute-start.2 = (bf16[4,8,64,128]{3,2,1,0:T(8,128)(2,1)S(1)}, bf16[4,8,64,128]{3,2,1,0:T(8,128)(2,1)S(1)}, u32[]{:S(2)}, u32[]{:S(2)}) collective-permute-start(bf16[4,8,64,128]{3,2,1,0:T(8,128)(2,1)S(1)} %pad_maximum_fusion.1), channel_id=1, source_target_pairs={{0,16},{4,20},{8,24},{12,28},{16,0},{20,4},{24,8},{28,12},{1,17},{... | collective-permute-start | bytes 1572872 | tf_op jit(solution)/shard_map/ppermute | solution.py:23
  178.8 6.4 %copy-start.5 = (bf16[64,64,256]{2,1,0:T(8,128)(2,1)S(1)}, bf16[64,64,256]{2,1,0:T(8,128)(2,1)}, u32[]{:S(2)}) copy-start(bf16[64,64,256]{2,1,0:T(8,128)(2,1)} %all-gather.3.cloned.1.call-done) | copy-start | bytes 6291460
  178.8 6.4 %copy-start.6 = (bf16[4096,128]{1,0:T(8,128)(2,1)S(1)}, bf16[4096,128]{1,0:T(8,128)(2,1)}, u32[]{:S(2)}) copy-start(bf16[4096,128]{1,0:T(8,128)(2,1)} %get-tuple-element.22) | copy-start | bytes 3145732
  200.5 4.8 %copy-start.3 = (bf16[64,128,256]{1,0,2:T(8,128)(2,1)S(1)}, bf16[64,128,256]{1,0,2:T(8,128)(2,1)}, u32[]{:S(2)}) copy-start(bf16[64,128,256]{1,0,2:T(8,128)(2,1)} %copy.20) | copy-start | bytes 12582916
  200.5 4.8 %copy-start.4 = (bf16[128,50,256]{0,1,2:T(8,128)(2,1)S(1)}, bf16[128,50,256]{0,1,2:T(8,128)(2,1)}, u32[]{:S(2)}) copy-start(bf16[128,50,256]{0,1,2:T(8,128)(2,1)} %copy.27) | copy-start | bytes 9830404
  205.3 42.3 %copy-start.7 = (bf16[128,50]{0,1:T(8,128)(2,1)S(1)}, bf16[128,50]{0,1:T(8,128)(2,1)}, u32[]{:S(2)}) copy-start(bf16[128,50]{0,1:T(8,128)(2,1)} %param.15) | copy-start | bytes 38404
  205.3 48.8 %copy-start.1 = (bf16[128,4096]{1,0:T(8,128)(2,1)S(1)}, bf16[128,4096]{1,0:T(8,128)(2,1)}, u32[]{:S(2)}) copy-start(bf16[128,4096]{1,0:T(8,128)(2,1)} %param.12) | copy-start | bytes 3145732
Sparse Core Ops, SparseCore 0:
  103.5 66.2 all-gather.2
  178.9 56.6 all-gather.4
